TPU v7x, 32 devices: a whole 2x2x4 slice. The times are simulated.
32 devices in a mesh: wide: 8 (over z, x), narrow: 4 (over y, core).
Axes of the slice: x: 2, y: 2, z: 4, core: 2. Of those that a mesh axis runs over, the one named last changes fastest.
Arguments:
- payload: bfloat16 [131072, 128], P(('wide', 'narrow')), may hold values from -6 to 6
- first_key: int32 [131072], P(('wide', 'narrow')), may hold values from 0 to 1073741823
- second_key: int32 [131072], P(('wide', 'narrow')), may hold values from 0 to 1073741823
- live: int32 [131072], P(('wide', 'narrow')), may hold values from 0 to 1
- first_bucket: int32 [131072], P(('wide', 'narrow')), may hold values from 0 to 7, as said below
- second_bucket: int32 [131072], P(('wide', 'narrow')), may hold values from 0 to 3
Outputs:
- group_mean: bfloat16 [131072, 128], P(('wide', 'narrow'))
- duplicate_count: int32 [], replicated
Inputs may be any that keep to these rules, and one draw needn't show every extreme that they name: Each device's rows name each pair (first_bucket, second_bucket) exactly 128 times; in every draw there is one bucket pair all of whose rows survive; other rows survive or not as `live` says.
All inputs are finite; a program needn't handle non-finite values.
Results may differ from a plain program's by a relative error of at most 0.001.
Values may be sent and summed in bfloat16 or wider, within the bound.
A program may use at most 64 MiB of HBM per device.

v0:
```python
import jax
import jax.numpy as jnp
from jax import lax
from jax.sharding import PartitionSpec as P


def pair_mask(row_one, row_two, row_live, col_one, col_two, col_live):
    return (
        (row_one[:, None] == col_one[None, :])
        & (row_two[:, None] == col_two[None, :])
        & (row_live[:, None] > 0)
        & (col_live[None, :] > 0)
    )


def on_device(payload, first_key, second_key, live, first_bucket, second_bucket):
    wide_count = lax.axis_size("wide")
    narrow_count = lax.axis_size("narrow")
    row_count, feature_cols = payload.shape
    slot_rows = row_count // (wide_count * narrow_count)
    owner = first_bucket * narrow_count + second_bucket
    sort_order = jnp.argsort(owner, stable=True)
    inverse = jnp.argsort(sort_order, stable=True)
    sent_rows = payload[sort_order].reshape(wide_count, narrow_count, slot_rows, feature_cols)
    shaped = (wide_count, narrow_count, slot_rows)
    tags = jnp.stack(
        [
            first_key[sort_order].reshape(shaped),
            second_key[sort_order].reshape(shaped),
            live[sort_order].reshape(shaped),
        ],
        axis=2,
    )
    got_rows, got_tags = (
        lax.all_to_all(
            lax.all_to_all(sent_rows, "wide", split_axis=0, concat_axis=0, tiled=True),
            "narrow",
            split_axis=1,
            concat_axis=1,
            tiled=True,
        ),
        lax.all_to_all(
            lax.all_to_all(tags, "wide", split_axis=0, concat_axis=0, tiled=True),
            "narrow",
            split_axis=1,
            concat_axis=1,
            tiled=True,
        ),
    )
    owner_rows = wide_count * narrow_count * slot_rows
    flat_rows = got_rows.reshape(owner_rows, feature_cols)
    keys_one = got_tags[:, :, 0, :].reshape(owner_rows)
    keys_two = got_tags[:, :, 1, :].reshape(owner_rows)
    alive = got_tags[:, :, 2, :].reshape(owner_rows)
    tile_rows = min(512, owner_rows)
    column_pos = lax.iota(jnp.int32, owner_rows)

    def full_block(block_index, running):
        group_means, duplicate_total = running
        block_start = block_index * tile_rows
        row_one = lax.dynamic_slice_in_dim(keys_one, block_start, tile_rows)
        row_two = lax.dynamic_slice_in_dim(keys_two, block_start, tile_rows)
        row_live = lax.dynamic_slice_in_dim(alive, block_start, tile_rows)
        same = pair_mask(row_one, row_two, row_live, keys_one, keys_two, alive)
        sums = jnp.dot(same.astype(jnp.bfloat16), flat_rows, preferred_element_type=jnp.float32)
        counts = jnp.sum(same.astype(jnp.float32), axis=1)
        row_pos = block_start + lax.iota(jnp.int32, tile_rows)
        earlier = same & (column_pos[None, :] < row_pos[:, None])
        duplicate_total = duplicate_total + jnp.sum(jnp.any(earlier, axis=1).astype(jnp.float32))
        block_mean = (sums / jnp.maximum(counts, 1.0)[:, None]).astype(jnp.bfloat16)
        group_means = lax.dynamic_update_slice_in_dim(group_means, block_mean, block_start, 0)
        return (group_means, duplicate_total)

    start_state = (jnp.zeros((owner_rows, feature_cols), jnp.bfloat16), jnp.zeros((), jnp.float32))
    group_means, duplicate_total = lax.fori_loop(
        0, owner_rows // tile_rows, full_block, start_state
    )
    back_rows = group_means.reshape(wide_count, narrow_count, slot_rows, feature_cols)
    returned = lax.all_to_all(
        lax.all_to_all(back_rows, "wide", split_axis=0, concat_axis=0, tiled=True),
        "narrow",
        split_axis=1,
        concat_axis=1,
        tiled=True,
    )
    group_mean = returned.reshape(row_count, feature_cols)[inverse]
    overall = lax.psum(duplicate_total, ("wide", "narrow"))
    return (group_mean, overall.astype(jnp.int32))


def solution(mesh):
    placed = (
        P(("wide", "narrow"), None),
        P(("wide", "narrow")),
        P(("wide", "narrow")),
        P(("wide", "narrow")),
        P(("wide", "narrow")),
        P(("wide", "narrow")),
    )
    return jax.shard_map(
        on_device,
        mesh=mesh,
        in_specs=placed,
        out_specs=(P(("wide", "narrow"), None), P()),
        check_vma=False,
    )
```

profile of v0, /device:TPU:0, one launch (start us, length us, event | category | flops | bytes accessed | tf_op | source)
XLA Modules:
  0.0 326.9 jit_solution(6354122044880662689)
XLA Ops:
  0.7 0.8 multiply_add_fusion
  1.5 5.8 %sort.31 = (s32[4096]{0:T(1024)}, s32[4096]{0:T(1024)S(1)}) sort(s32[4096]{0:T(1024)S(1)} %multiply_add_fusion, s32[4096]{0:T(1024)S(1)} %iota.19), dimensions={0}, to_apply=%region_0.0 | sort | flops 49152 | bytes 65536 | tf_op jit(solution)/shard_map/jit(argsort)/sort | solution.py:22
  7.3 23.0 %gather_fusion.2 = s32[4096]{0:T(1024)S(1)} fusion(s32[4096]{0:T(1024)S(1)} %copy-done.1, s32[4096]{0:T(1024)S(1)} %fusion.6), kind=kCustom, calls=%fused_computation.2 | custom fusion | bytes 49152 | tf_op jit(solution)/shard_map/gather | solution.py:30
  30.4 23.0 %gather_fusion.1 = s32[4096]{0:T(1024)S(1)} fusion(s32[4096]{0:T(1024)S(1)} %copy-done.2, s32[4096]{0:T(1024)S(1)} %fusion.6), kind=kCustom, calls=%fused_computation.1 | custom fusion | bytes 49152 | tf_op jit(solution)/shard_map/gather | solution.py:29
  53.4 23.0 %gather_fusion = s32[4096]{0:T(1024)S(1)} fusion(s32[4096]{0:T(1024)S(1)} %copy-done.3, s32[4096]{0:T(1024)S(1)} %fusion.6), kind=kCustom, calls=%fused_computation | custom fusion | bytes 49152 | tf_op jit(solution)/shard_map/gather | solution.py:28
  77.1 7.3 %all-to-all-start = ((s32[8,4,3,128]{3,1,2,0:T(4,128)}), s32[8,4,3,128]{3,1,2,0:T(4,128)S(1)}, u32[]{:S(2)}, u32[]{:S(2)}) async-start(s32[8,4,3,128]{3,1,2,0:T(4,128)} %pad_add_fusion), calls=%async_computation | async-start | bytes 98304 | tf_op jit(solution)/shard_map/all_to_all | solution.py:43
  84.4 15.0 %gather_fusion.3 = bf16[4096,128]{1,0:T(8,128)(2,1)} fusion(bf16[4096,128]{1,0:T(8,128)(2,1)S(1)} %copy-done, s32[4096]{0:T(1024)S(1)} %fusion.6), kind=kCustom, calls=%fused_computation.3 | custom fusion | bytes 2113536 | tf_op jit(solution)/shard_map/gather | solution.py:24
  99.4 6.0 %all-to-all-start.2 = ((bf16[8,4,128,128]{3,2,1,0:T(8,128)(2,1)}), bf16[8,4,128,128]{3,2,1,0:T(8,128)(2,1)S(1)}, u32[]{:S(2)}, u32[]{:S(2)}) async-start(bf16[8,4,128,128]{3,2,1,0:T(8,128)(2,1)} %bitcast.6), calls=%async_computation.2 | async-start | bytes 2097152 | tf_op jit(solution)/shard_map/all_to_all | solution.py:36
  106.0 24.8 %all-to-all-done.2 = bf16[8,4,128,128]{3,2,1,0:T(8,128)(2,1)S(1)} async-done(((bf16[8,4,128,128]{3,2,1,0:T(8,128)(2,1)}), bf16[8,4,128,128]{3,2,1,0:T(8,128)(2,1)S(1)}, u32[]{:S(2)}, u32[]{:S(2)}) %all-to-all-start.2) | async-done | bytes 1048608 | tf_op jit(solution)/shard_map/all_to_all | solution.py:36
  130.8 3.3 %all-to-all-start.1 = ((s32[8,4,3,128]{3,0,2,1:T(8,128)}), s32[8,4,3,128]{3,0,2,1:T(8,128)S(1)}, u32[]{:S(2)}, u32[]{:S(2)}) async-start(s32[8,4,3,128]{3,0,2,1:T(8,128)} %copy.38), calls=%async_computation.1 | async-start | bytes 98304 | tf_op jit(solution)/shard_map/all_to_all | solution.py:42
  134.1 1.0 copy.42
  135.1 3.0 all-to-all-done.1
  138.1 3.5 %all-to-all-start.3 = ((bf16[8,4,128,128]{3,2,0,1:T(8,128)(2,1)}), bf16[8,4,128,128]{3,2,0,1:T(8,128)(2,1)S(1)}, u32[]{:S(2)}, u32[]{:S(2)}) async-start(bf16[8,4,128,128]{3,2,0,1:T(8,128)(2,1)} %copy.42), calls=%async_computation.3 | async-start | bytes 2097152 | tf_op jit(solution)/shard_map/all_to_all | solution.py:35
  141.7 14.3 %all-to-all-done.3 = bf16[8,4,128,128]{3,2,0,1:T(8,128)(2,1)S(1)} async-done(((bf16[8,4,128,128]{3,2,0,1:T(8,128)(2,1)}), bf16[8,4,128,128]{3,2,0,1:T(8,128)(2,1)S(1)}, u32[]{:S(2)}, u32[]{:S(2)}) %all-to-all-start.3) | async-done | bytes 1048608 | tf_op jit(solution)/shard_map/all_to_all | solution.py:35
  156.0 1.1 copy.43
  157.1 1.1 broadcast_in_dim.30
  158.2 71.2 %while.16 = (s32[]{:T(128)}, bf16[4096,128]{1,0:T(8,128)(2,1)}, f32[]{:T(128)}, s32[4096]{0:T(1024)S(1)}, s32[8,4,1,128]{3,2,1,0:T(1,128)S(1)}, /*index=5*/s32[4...) while((s32[]{:T(128)}, bf16[4096,128]{1,0:T(8,128)(2,1)}, ...), condition=%wide.region_5.6_spmd.clone, body=%wide.region_1.5_spmd.clone.sunk | while | flops 557979136 | bytes 11751667 | solution.py:75
  158.4 4.1 %fusion.17 = (pred[512]{0:T(512)(128)(4,1)S(1)}, pred[512,4096]{1,0:T(32,128)(4,1)S(1)}) fusion(s32[512]{0:T(512)S(1)} %iota_add_fusion.2, pred[4096]{0:T(1024)(128)(4,1)S(1)} %bitcast.33, pred[512]{0:T(512)(128)(4,1)S(1)} %dynamic-slice_compare_fusion.2, s32[4096]{0:T(1024)S(1)} %bitcast.31, s32[512]{0:T(512)S(1)} %dynamic_slice.29, ...), kind=kLoop, calls=%fused_computation.9.clone.1 | loop fusion | flops 16776704 | bytes 2141184 | tf_op jit(solution)/shard_map/while/body/eval_jaxpr/reduce_or | solution.py:69
  162.6 0.7 convert_reduce_fusion.5
  164.0 1.0 convert_reduce_fusion.4
  165.2 1.9 fusion.18
  167.3 4.1 %fusion.17 = (pred[512]{0:T(512)(128)(4,1)S(1)}, pred[512,4096]{1,0:T(32,128)(4,1)S(1)}) fusion(s32[512]{0:T(512)S(1)} %iota_add_fusion.2, pred[4096]{0:T(1024)(128)(4,1)S(1)} %bitcast.33, pred[512]{0:T(512)(128)(4,1)S(1)} %dynamic-slice_compare_fusion.2, s32[4096]{0:T(1024)S(1)} %bitcast.31, s32[512]{0:T(512)S(1)} %dynamic_slice.29, ...), kind=kLoop, calls=%fused_computation.9.clone.1 | loop fusion | flops 16776704 | bytes 2141184 | tf_op jit(solution)/shard_map/while/body/eval_jaxpr/reduce_or | solution.py:69
  172.9 1.0 convert_reduce_fusion.4
  174.1 1.9 fusion.18
  176.2 4.1 %fusion.17 = (pred[512]{0:T(512)(128)(4,1)S(1)}, pred[512,4096]{1,0:T(32,128)(4,1)S(1)}) fusion(s32[512]{0:T(512)S(1)} %iota_add_fusion.2, pred[4096]{0:T(1024)(128)(4,1)S(1)} %bitcast.33, pred[512]{0:T(512)(128)(4,1)S(1)} %dynamic-slice_compare_fusion.2, s32[4096]{0:T(1024)S(1)} %bitcast.31, s32[512]{0:T(512)S(1)} %dynamic_slice.29, ...), kind=kLoop, calls=%fused_computation.9.clone.1 | loop fusion | flops 16776704 | bytes 2141184 | tf_op jit(solution)/shard_map/while/body/eval_jaxpr/reduce_or | solution.py:69
  181.8 1.0 convert_reduce_fusion.4
  183.0 1.9 fusion.18
  185.1 4.1 %fusion.17 = (pred[512]{0:T(512)(128)(4,1)S(1)}, pred[512,4096]{1,0:T(32,128)(4,1)S(1)}) fusion(s32[512]{0:T(512)S(1)} %iota_add_fusion.2, pred[4096]{0:T(1024)(128)(4,1)S(1)} %bitcast.33, pred[512]{0:T(512)(128)(4,1)S(1)} %dynamic-slice_compare_fusion.2, s32[4096]{0:T(1024)S(1)} %bitcast.31, s32[512]{0:T(512)S(1)} %dynamic_slice.29, ...), kind=kLoop, calls=%fused_computation.9.clone.1 | loop fusion | flops 16776704 | bytes 2141184 | tf_op jit(solution)/shard_map/while/body/eval_jaxpr/reduce_or | solution.py:69
  190.7 1.0 convert_reduce_fusion.4
  191.9 1.9 fusion.18
  194.0 4.1 %fusion.17 = (pred[512]{0:T(512)(128)(4,1)S(1)}, pred[512,4096]{1,0:T(32,128)(4,1)S(1)}) fusion(s32[512]{0:T(512)S(1)} %iota_add_fusion.2, pred[4096]{0:T(1024)(128)(4,1)S(1)} %bitcast.33, pred[512]{0:T(512)(128)(4,1)S(1)} %dynamic-slice_compare_fusion.2, s32[4096]{0:T(1024)S(1)} %bitcast.31, s32[512]{0:T(512)S(1)} %dynamic_slice.29, ...), kind=kLoop, calls=%fused_computation.9.clone.1 | loop fusion | flops 16776704 | bytes 2141184 | tf_op jit(solution)/shard_map/while/body/eval_jaxpr/reduce_or | solution.py:69
  199.6 1.0 convert_reduce_fusion.4
  200.8 1.9 fusion.18
  202.9 4.1 %fusion.17 = (pred[512]{0:T(512)(128)(4,1)S(1)}, pred[512,4096]{1,0:T(32,128)(4,1)S(1)}) fusion(s32[512]{0:T(512)S(1)} %iota_add_fusion.2, pred[4096]{0:T(1024)(128)(4,1)S(1)} %bitcast.33, pred[512]{0:T(512)(128)(4,1)S(1)} %dynamic-slice_compare_fusion.2, s32[4096]{0:T(1024)S(1)} %bitcast.31, s32[512]{0:T(512)S(1)} %dynamic_slice.29, ...), kind=kLoop, calls=%fused_computation.9.clone.1 | loop fusion | flops 16776704 | bytes 2141184 | tf_op jit(solution)/shard_map/while/body/eval_jaxpr/reduce_or | solution.py:69
  208.5 1.0 convert_reduce_fusion.4
  209.7 1.9 fusion.18
  211.9 4.1 %fusion.17 = (pred[512]{0:T(512)(128)(4,1)S(1)}, pred[512,4096]{1,0:T(32,128)(4,1)S(1)}) fusion(s32[512]{0:T(512)S(1)} %iota_add_fusion.2, pred[4096]{0:T(1024)(128)(4,1)S(1)} %bitcast.33, pred[512]{0:T(512)(128)(4,1)S(1)} %dynamic-slice_compare_fusion.2, s32[4096]{0:T(1024)S(1)} %bitcast.31, s32[512]{0:T(512)S(1)} %dynamic_slice.29, ...), kind=kLoop, calls=%fused_computation.9.clone.1 | loop fusion | flops 16776704 | bytes 2141184 | tf_op jit(solution)/shard_map/while/body/eval_jaxpr/reduce_or | solution.py:69
  217.4 1.0 convert_reduce_fusion.4
  218.6 1.9 fusion.18
  220.8 4.1 %fusion.17 = (pred[512]{0:T(512)(128)(4,1)S(1)}, pred[512,4096]{1,0:T(32,128)(4,1)S(1)}) fusion(s32[512]{0:T(512)S(1)} %iota_add_fusion.2, pred[4096]{0:T(1024)(128)(4,1)S(1)} %bitcast.33, pred[512]{0:T(512)(128)(4,1)S(1)} %dynamic-slice_compare_fusion.2, s32[4096]{0:T(1024)S(1)} %bitcast.31, s32[512]{0:T(512)S(1)} %dynamic_slice.29, ...), kind=kLoop, calls=%fused_computation.9.clone.1 | loop fusion | flops 16776704 | bytes 2141184 | tf_op jit(solution)/shard_map/while/body/eval_jaxpr/reduce_or | solution.py:69
  226.3 1.0 convert_reduce_fusion.4
  227.5 1.9 fusion.18
  229.4 29.2 %all_to_all.30 = bf16[8,4,128,128]{3,2,1,0:T(8,128)(2,1)S(1)} all-to-all(bf16[8,4,128,128]{3,2,1,0:T(8,128)(2,1)} %bitcast.26), channel_id=1, replica_groups=mesh['wide'=8,'narrow'=4] {'wide'}, dimensions={0} | all-to-all | bytes 2097152 | tf_op jit(solution)/shard_map/all_to_all | solution.py:80
  258.6 1.0 copy.47
  259.7 3.5 %all-to-all-start.5 = ((bf16[8,4,128,128]{3,2,0,1:T(8,128)(2,1)}), bf16[8,4,128,128]{3,2,0,1:T(8,128)(2,1)S(1)}, u32[]{:S(2)}, u32[]{:S(2)}) async-start(bf16[8,4,128,128]{3,2,0,1:T(8,128)(2,1)} %copy.47), calls=%async_computation.5 | async-start | bytes 2097152 | tf_op jit(solution)/shard_map/all_to_all | solution.py:79
  263.2 5.8 %sort.32 = (s32[4096]{0:T(1024)}, s32[4096]{0:T(1024)S(1)}) sort(s32[4096]{0:T(1024)S(1)} %get-tuple-element.189, s32[4096]{0:T(1024)S(1)} %iota.21), dimensions={0}, to_apply=%region_6.7 | sort | flops 49152 | bytes 65536 | tf_op jit(solution)/shard_map/jit(argsort)/sort | solution.py:23
  269.0 40.9 %psum.7 = f32[]{:T(128)} all-reduce(f32[]{:T(128)} %get-tuple-element.192), channel_id=1, replica_groups=mesh['wide'=8,'narrow'=4] {'wide','narrow'}, use_global_device_ids=true, to_apply=%region_7.8 | all-reduce | flops 1 | bytes 8 | tf_op jit(solution)/shard_map/psum | solution.py:87
  310.7 15.0 %gather_fusion.4 = bf16[4096,128]{1,0:T(8,128)(2,1)} fusion(bf16[4096,128]{1,0:T(8,128)(2,1)S(1)} %bitcast.25, s32[4096]{0:T(1024)S(1)} %fusion.7), kind=kCustom, calls=%fused_computation.4 | custom fusion | bytes 2113536 | tf_op jit(solution)/shard_map/gather | solution.py:86
  (94 shorter events, 10.1 us)
Async XLA Ops:
  0.6 83.7 %copy-start = (bf16[4096,128]{1,0:T(8,128)(2,1)S(1)}, bf16[4096,128]{1,0:T(8,128)(2,1)}, u32[]{:S(2)}) copy-start(bf16[4096,128]{1,0:T(8,128)(2,1)} %param.8) | copy-start | bytes 3145732
  0.6 6.6 %copy-start.1 = (s32[4096]{0:T(1024)S(1)}, s32[4096]{0:T(1024)}, u32[]{:S(2)}) copy-start(s32[4096]{0:T(1024)} %param.11) | copy-start | bytes 49156
  7.3 23.1 %copy-start.2 = (s32[4096]{0:T(1024)S(1)}, s32[4096]{0:T(1024)}, u32[]{:S(2)}) copy-start(s32[4096]{0:T(1024)} %param.10) | copy-start | bytes 49156
  30.3 23.1 %copy-start.3 = (s32[4096]{0:T(1024)S(1)}, s32[4096]{0:T(1024)}, u32[]{:S(2)}) copy-start(s32[4096]{0:T(1024)} %param.9) | copy-start | bytes 49156
  77.1 22.3 %all-to-all-start = ((s32[8,4,3,128]{3,1,2,0:T(4,128)}), s32[8,4,3,128]{3,1,2,0:T(4,128)S(1)}, u32[]{:S(2)}, u32[]{:S(2)}) async-start(s32[8,4,3,128]{3,1,2,0:T(4,128)} %pad_add_fusion), calls=%async_computation | async-start | bytes 98304 | tf_op jit(solution)/shard_map/all_to_all | solution.py:43
  99.4 31.4 %all-to-all-start.2 = ((bf16[8,4,128,128]{3,2,1,0:T(8,128)(2,1)}), bf16[8,4,128,128]{3,2,1,0:T(8,128)(2,1)S(1)}, u32[]{:S(2)}, u32[]{:S(2)}) async-start(bf16[8,4,128,128]{3,2,1,0:T(8,128)(2,1)} %bitcast.6), calls=%async_computation.2 | async-start | bytes 2097152 | tf_op jit(solution)/shard_map/all_to_all | solution.py:36
  130.8 7.3 %all-to-all-start.1 = ((s32[8,4,3,128]{3,0,2,1:T(8,128)}), s32[8,4,3,128]{3,0,2,1:T(8,128)S(1)}, u32[]{:S(2)}, u32[]{:S(2)}) async-start(s32[8,4,3,128]{3,0,2,1:T(8,128)} %copy.38), calls=%async_computation.1 | async-start | bytes 98304 | tf_op jit(solution)/shard_map/all_to_all | solution.py:42
  138.1 17.9 %all-to-all-start.3 = ((bf16[8,4,128,128]{3,2,0,1:T(8,128)(2,1)}), bf16[8,4,128,128]{3,2,0,1:T(8,128)(2,1)S(1)}, u32[]{:S(2)}, u32[]{:S(2)}) async-start(bf16[8,4,128,128]{3,2,0,1:T(8,128)(2,1)} %copy.42), calls=%async_computation.3 | async-start | bytes 2097152 | tf_op jit(solution)/shard_map/all_to_all | solution.py:35
  163.9 1.2 copy-start.4
  172.8 1.2 copy-start.4
  181.8 1.2 copy-start.4
  190.7 1.2 copy-start.4
  199.6 1.2 copy-start.4
  208.5 1.2 copy-start.4
  217.4 1.2 copy-start.4
  226.3 1.2 copy-start.4
  259.7 50.9 %all-to-all-start.5 = ((bf16[8,4,128,128]{3,2,0,1:T(8,128)(2,1)}), bf16[8,4,128,128]{3,2,0,1:T(8,128)(2,1)S(1)}, u32[]{:S(2)}, u32[]{:S(2)}) async-start(bf16[8,4,128,128]{3,2,0,1:T(8,128)(2,1)} %copy.47), calls=%async_computation.5 | async-start | bytes 2097152 | tf_op jit(solution)/shard_map/all_to_all | solution.py:79
where the time goes:
time: 328 us; the launch traced here: 327 us
  local copies, waits for them, and re-layouts  107 us (33%)
  blocking collectives  70.1 us (21%)
  other arithmetic  60 us (18%)
  waiting for transfers between devices  42.1 us (13%)
  starting transfers between devices  23.6 us (7%)
  matrix products  15.4 us (5%)
  loops' own time  5.75 us (2%)
    psum x1, blocking collectives, on_device(): overall = lax.psum(duplicate_total, ('wide', 'narrow'))  40.9 us
    reduce_or x8, other arithmetic, full_block(): jnp.any(earlier, axis=1).astype(jnp.float32)  33 us
    all_to_all x1, blocking collectives, on_device(): lax.all_to_all(back_rows, 'wide', split_axis=0, concat_axis=0, tiled=True)  29.2 us
    all_to_all x1, waiting for transfers between devices, on_device(): lax.all_to_all(sent_rows, 'wide', split_axis=0, concat_axis=0, tiled=True)  24.8 us
    gather x1, local copies, waits for them, and re-layouts, on_device(): live[sort_order].reshape(shaped)  23 us
    gather x1, local copies, waits for them, and re-layouts, on_device(): second_key[sort_order].reshape(shaped)  23 us
    gather x1, local copies, waits for them, and re-layouts, on_device(): first_key[sort_order].reshape(shaped)  23 us
    dot_general x8, matrix products, full_block(): jnp.dot(same.astype(jnp.bfloat16), flat_rows, preferred_element_type=jnp....  15.4 us
  transfers between devices with their start and end apart: 5, of which 3 were waited for; matrix products, arithmetic and copies ran while one was open for 7% of the time, Pallas kernels for 0%

commit v1 on v0

v1 whole, which is shorter than its diff:
```python
import functools

import jax
import jax.numpy as jnp
from jax import lax
from jax.experimental import pallas as pl
from jax.experimental.pallas import tpu as pltpu
from jax.sharding import PartitionSpec as P

MESH = pl.DeviceIdType.MESH
VMEM = pltpu.VMEM
SMEM = pltpu.SMEM


def place(flat, narrow_count):
    return {"wide": flat // narrow_count, "narrow": flat % narrow_count}


def my_flat(narrow_count):
    return lax.axis_index("wide") * narrow_count + lax.axis_index("narrow")


def greet_all(me, devices, narrow_count):
    barrier = pltpu.get_barrier_semaphore()

    def greet(step, carry):
        peer = (me + step) % devices
        pl.semaphore_signal(
            barrier, inc=1, device_id=place(peer, narrow_count), device_id_type=MESH
        )
        return carry

    lax.fori_loop(1, devices, greet, 0)
    pl.semaphore_wait(barrier, devices - 1)


def wait_bytes(ref, sem):
    pltpu.make_async_copy(ref, ref, sem).wait()


def send_block(src, dst, send_sem, recv_sem, peer, narrow_count):
    pltpu.make_async_remote_copy(
        src_ref=src,
        dst_ref=dst,
        send_sem=send_sem,
        recv_sem=recv_sem,
        device_id=place(peer, narrow_count),
        device_id_type=MESH,
    ).start()


def tags_kernel(devices, narrow_count, tags_ref, got_ref, send_sem, recv_sem):
    me = my_flat(narrow_count)
    greet_all(me, devices, narrow_count)
    pltpu.make_async_copy(tags_ref.at[me], got_ref.at[me], recv_sem).start()

    def send(step, carry):
        peer = (me + step) % devices
        send_block(tags_ref.at[peer], got_ref.at[me], send_sem, recv_sem, peer, narrow_count)
        return carry

    lax.fori_loop(1, devices, send, 0)
    wait_bytes(got_ref, recv_sem)
    wait_bytes(tags_ref.at[pl.ds(0, devices - 1)], send_sem)


def gather_kernel(unroll, order_ref, rows_ref, out_ref, wide_in, wide_out):
    count = rows_ref.shape[0]
    wide_in[...] = rows_ref[...].astype(jnp.float32)

    def move(step, carry):
        base = pl.multiple_of(step * unroll, unroll)
        for u in range(unroll):
            source = order_ref[base + u]
            wide_out[pl.ds(base + u, 1), :] = wide_in[pl.ds(source, 1), :]
        return carry

    lax.fori_loop(0, count // unroll, move, 0)
    out_ref[...] = wide_out[...].astype(out_ref.dtype)


def scatter_kernel(unroll, order_ref, rows_ref, out_ref, wide_in, wide_out):
    count = rows_ref.shape[0]
    wide_in[...] = rows_ref[...].astype(jnp.float32)

    def move(step, carry):
        base = pl.multiple_of(step * unroll, unroll)
        for u in range(unroll):
            target = order_ref[base + u]
            wide_out[pl.ds(target, 1), :] = wide_in[pl.ds(base + u, 1), :]
        return carry

    lax.fori_loop(0, count // unroll, move, 0)
    out_ref[...] = wide_out[...].astype(out_ref.dtype)


def permute_rows(kernel, order, rows):
    count, cols = rows.shape
    return pl.pallas_call(
        functools.partial(kernel, 16),
        out_shape=jax.ShapeDtypeStruct(rows.shape, rows.dtype),
        in_specs=[pl.BlockSpec(memory_space=SMEM), pl.BlockSpec(memory_space=VMEM)],
        out_specs=pl.BlockSpec(memory_space=VMEM),
        scratch_shapes=[VMEM((count, cols), jnp.float32), VMEM((count, cols), jnp.float32)],
    )(order, rows)


def exchange_kernel(
    devices, narrow_count, chunks, tile,
    rows_ref, key_one_ref, key_two_ref,
    back_ref, dup_ref,
    got, totals, means, col_one, col_two, lane_one, wide_rows, dup_mine, dup_all,
    send_sem, recv_sems, back_send, back_recv, dup_send, dup_recv,
):
    _, slot_rows, cols = rows_ref.shape
    count = devices * slot_rows
    chunk_slots = devices // chunks
    chunk_rows = chunk_slots * slot_rows
    lanes = key_one_ref.shape[1]
    me = my_flat(narrow_count)
    my_chunk = me // chunk_slots
    greet_all(me, devices, narrow_count)

    pltpu.make_async_copy(rows_ref.at[me], got.at[me], recv_sems.at[0]).start()
    for c in range(chunks):
        first = ((my_chunk + c) % chunks) * chunk_slots

        def send(step, carry, first=first, c=c):
            peer = first + (me + step) % chunk_slots
            send_block(
                rows_ref.at[peer], got.at[me], send_sem, recv_sems.at[c], peer, narrow_count
            )
            return carry

        lax.fori_loop(1 if c == 0 else 0, chunk_slots, send, 0)

    one = key_one_ref[...]
    lane_one[...] = jnp.where(one < 0, -2, one)
    flipped_one = one.T
    flipped_two = key_two_ref[...].T
    for r in range(count // lanes):
        at = pl.ds(r * lanes, lanes)
        col_one[at, :] = jnp.broadcast_to(flipped_one[:, r : r + 1], (lanes, lanes))
        col_two[at, :] = jnp.broadcast_to(flipped_two[:, r : r + 1], (lanes, lanes))
    wide_rows[:, cols:] = jnp.ones((chunk_rows, cols), wide_rows.dtype)
    dup_mine[...] = jnp.zeros_like(dup_mine)

    tiles = count // tile
    tile_slots = tile // slot_rows
    my_tile = me // tile_slots

    def send_tile(index):
        for u in range(tile_slots):
            peer = index * tile_slots + u

            @pl.when(peer == me)
            def _():
                pltpu.make_async_copy(means.at[peer], back_ref.at[me], back_recv).start()

            @pl.when(peer != me)
            def _():
                send_block(
                    means.at[peer], back_ref.at[me], back_send, back_recv, peer, narrow_count
                )

    for c in range(chunks):
        first = ((my_chunk - c + chunks) % chunks) * chunk_slots
        wait_bytes(got.at[pl.ds(first, chunk_slots)], recv_sems.at[c])
        wide_rows[:, :cols] = got[pl.ds(first, chunk_slots)].reshape(chunk_rows, cols)
        lane_base = first * slot_rows // lanes

        def body(step, carry, c=c, lane_base=lane_base):
            index = (my_tile + step) % tiles
            at = pl.ds(pl.multiple_of(index * tile, tile), tile)
            left_one = col_one[at, :]
            left_two = col_two[at, :]
            parts = []
            for b in range(chunk_rows // lanes):
                row_at = pl.ds(lane_base + b, 1)
                same = (left_one == lane_one[row_at, :]) & (left_two == key_two_ref[row_at, :])
                parts.append(jnp.where(same, 1.0, 0.0).astype(jnp.bfloat16))
            mask = jnp.concatenate(parts, axis=1)
            part = jnp.dot(mask, wide_rows[...], preferred_element_type=jnp.float32)
            if c > 0:
                part = part + totals[at, :]
            if c < chunks - 1:
                totals[at, :] = part
            else:
                sums = part[:, :cols]
                counts = part[:, cols:]
                floor = jnp.maximum(counts, 1.0)
                mean = (sums / floor).astype(means.dtype)
                means[pl.ds(index * tile_slots, tile_slots)] = mean.reshape(
                    tile_slots, slot_rows, cols
                )
                held = jnp.where(counts > 0.0, 1.0, 0.0)
                dup_mine[0] += jnp.sum(held.reshape(tile // 8, 8, cols), axis=0)
                dup_mine[1] += jnp.sum((held / floor).reshape(tile // 8, 8, cols), axis=0)

                @pl.when(step > 0)
                def _():
                    send_tile((my_tile + step + tiles - 1) % tiles)
            return carry

        lax.fori_loop(0, tiles, body, 0)

    live_rows = jnp.sum(dup_mine[0], axis=0, keepdims=True)
    groups = jnp.floor(jnp.sum(dup_mine[1], axis=0, keepdims=True) + 0.5)
    dup_mine[0] = jnp.broadcast_to(live_rows - groups, (8, cols))
    send_tile((my_tile + tiles - 1) % tiles)
    pltpu.make_async_copy(dup_mine.at[0], dup_all.at[me], dup_recv).start()

    def send_dup(step, carry):
        peer = (me + step) % devices
        send_block(dup_mine.at[0], dup_all.at[me], dup_send, dup_recv, peer, narrow_count)
        return carry

    lax.fori_loop(1, devices, send_dup, 0)
    wait_bytes(dup_all, dup_recv)
    dup_ref[...] = jnp.sum(dup_all[...], axis=0).astype(jnp.int32)
    wait_bytes(back_ref, back_recv)
    wait_bytes(rows_ref.at[pl.ds(0, devices - 1)], send_sem)
    wait_bytes(means.at[pl.ds(0, devices - 1)], back_send)
    wait_bytes(dup_all.at[pl.ds(0, devices - 1)], dup_send)


def on_device(payload, first_key, second_key, live, first_bucket, second_bucket):
    wide_count = lax.axis_size("wide")
    narrow_count = lax.axis_size("narrow")
    devices = wide_count * narrow_count
    row_count, cols = payload.shape
    slot_rows = row_count // devices
    owner = first_bucket * narrow_count + second_bucket
    packed = owner * row_count + lax.iota(jnp.int32, row_count)
    packed, key_one, key_two = lax.sort(
        (packed, jnp.where(live > 0, first_key, -1), second_key), num_keys=1, is_stable=False
    )
    order = packed % row_count
    tags = jnp.stack(
        [key_one.reshape(devices, slot_rows), key_two.reshape(devices, slot_rows)], axis=1
    ).reshape(devices, 1, 2 * slot_rows)
    got_tags = pl.pallas_call(
        functools.partial(tags_kernel, devices, narrow_count),
        out_shape=jax.ShapeDtypeStruct(tags.shape, tags.dtype),
        in_specs=[pl.BlockSpec(memory_space=VMEM)],
        out_specs=pl.BlockSpec(memory_space=VMEM),
        scratch_shapes=[pltpu.SemaphoreType.DMA, pltpu.SemaphoreType.DMA],
        compiler_params=pltpu.CompilerParams(collective_id=0, has_side_effects=True),
    )(tags)
    lanes = 128
    keys_one = got_tags[:, 0, :slot_rows].reshape(row_count // lanes, lanes)
    keys_two = got_tags[:, 0, slot_rows:].reshape(row_count // lanes, lanes)
    sent = permute_rows(gather_kernel, order, payload).reshape(devices, slot_rows, cols)

    chunks = 4 if devices % 4 == 0 else 1
    tile = max(256, slot_rows)
    tile = min(tile, row_count)
    block = (devices, slot_rows, cols)
    back, dups = pl.pallas_call(
        functools.partial(exchange_kernel, devices, narrow_count, chunks, tile),
        out_shape=(
            jax.ShapeDtypeStruct(block, payload.dtype),
            jax.ShapeDtypeStruct((8, cols), jnp.int32),
        ),
        in_specs=[pl.BlockSpec(memory_space=VMEM)] * 3,
        out_specs=(pl.BlockSpec(memory_space=VMEM), pl.BlockSpec(memory_space=VMEM)),
        scratch_shapes=[
            VMEM(block, payload.dtype),
            VMEM((row_count, 2 * cols), jnp.float32),
            VMEM(block, payload.dtype),
            VMEM((row_count, lanes), jnp.int32),
            VMEM((row_count, lanes), jnp.int32),
            VMEM((row_count // lanes, lanes), jnp.int32),
            VMEM((row_count // chunks, 2 * cols), payload.dtype),
            VMEM((2, 8, cols), jnp.float32),
            VMEM((devices, 8, cols), jnp.float32),
            pltpu.SemaphoreType.DMA,
            pltpu.SemaphoreType.DMA((chunks,)),
            pltpu.SemaphoreType.DMA,
            pltpu.SemaphoreType.DMA,
            pltpu.SemaphoreType.DMA,
            pltpu.SemaphoreType.DMA,
        ],
        compiler_params=pltpu.CompilerParams(
            collective_id=1, has_side_effects=True, vmem_limit_bytes=48 * 1024 * 1024
        ),
    )(sent, keys_one, keys_two)
    group_mean = permute_rows(scatter_kernel, order, back.reshape(row_count, cols))
    return (group_mean, dups[0, 0])


def solution(mesh):
    placed = (
        P(("wide", "narrow"), None),
        P(("wide", "narrow")),
        P(("wide", "narrow")),
        P(("wide", "narrow")),
        P(("wide", "narrow")),
        P(("wide", "narrow")),
    )
    return jax.shard_map(
        on_device,
        mesh=mesh,
        in_specs=placed,
        out_specs=(P(("wide", "narrow"), None), P()),
        check_vma=False,
    )
```

time: 328 us -> 95 us (0.29)
  local copies, waits for them, and re-layouts: 107 us -> 3.46 us
  Pallas kernels: 0 us -> 83.3 us
  blocking collectives: 70.1 us -> 0 us
  other arithmetic: 60 us -> 7.02 us
  waiting for transfers between devices: 42.1 us -> 0 us
  starting transfers between devices: 23.6 us -> 0 us
  matrix products: 15.4 us -> 0 us
  loops' own time: 5.75 us -> 0 us
    gather x5 -> x0, local copies, waits for them, and re-layouts: 99.2 us -> none  [the longest x1 23 us: on_device(): live[sort_order].reshape(shaped)]
    pallas_call x0 -> x4, Pallas kernels: none -> 83.3 us  [the longest x1 58.8 us: on_device(): pl.pallas_call(functools.partial(exchange_kernel, devices, narrow_count,...]
    all_to_all x5 -> x0, waiting for transfers between devices: 42.1 us -> none  [the longest x1 24.8 us: on_device(): lax.all_to_all(sent_rows, 'wide', split_axis=0, concat_axis=0, tiled=True)]
    psum x1 -> x0, blocking collectives: 40.9 us -> none  [on_device(): overall = lax.psum(duplicate_total, ('wide', 'narrow'))]
    reduce_or x8 -> x0, other arithmetic: 33 us -> none  [full_block(): jnp.any(earlier, axis=1).astype(jnp.float32)]
    all_to_all x1 -> x0, blocking collectives: 29.2 us -> none  [on_device(): lax.all_to_all(back_rows, 'wide', split_axis=0, concat_axis=0, tiled=True)]
    all_to_all x5 -> x0, starting transfers between devices: 23.6 us -> none  [the longest x1 7.28 us: on_device(): lax.all_to_all(tags, 'wide', split_axis=0, concat_axis=0, tiled=True)]
    dot_general x8 -> x0, matrix products: 15.4 us -> none  [full_block(): jnp.dot(same.astype(jnp.bfloat16), flat_rows, preferred_element_type=jnp....]
  transfers between devices with their start and end apart: 5 -> 0, of which waited for: 3 -> 0; matrix products, arithmetic and copies ran while one was open for 7% -> 0% of each run, Pallas kernels for 0% -> 0%
where the time goes in v1:
time: 95 us; the launch traced here: 94.5 us
  Pallas kernels  83.3 us (88%)
  other arithmetic  7.02 us (7%)
  local copies, waits for them, and re-layouts  3.46 us (4%)
    pallas_call x1, Pallas kernels, on_device(): pl.pallas_call(functools.partial(exchange_kernel, devices, narrow_count,...  58.8 us
    pallas_call x2, Pallas kernels, permute_rows(): pl.pallas_call(functools.partial(kernel, 16), out_shape=jax.ShapeDtypeStr...  13.8 us
    pallas_call x1, Pallas kernels, on_device(): pl.pallas_call(functools.partial(tags_kernel, devices, narrow_count), out...  10.8 us
    sort x1, other arithmetic, on_device(): lax.sort((packed, jnp.where(live > 0, first_key, -1), second_key), num_ke...  4.98 us
    unnamed x6, local copies, waits for them, and re-layouts  2.21 us

profile of v1, /device:TPU:0, one launch (start us, length us, event | category | flops | bytes accessed | tf_op | source)
XLA Modules:
  0.0 94.5 jit_solution(11648581664846054559)
XLA Ops:
  0.6 0.0 copy-start.2
  0.6 0.8 iota_add_fusion
  1.4 0.0 copy-done.2
  1.4 5.0 %sort.21 = (s32[4096]{0:T(1024)S(1)}, s32[4096]{0:T(1024)S(1)}, s32[4096]{0:T(1024)S(1)}) sort(s32[4096]{0:T(1024)S(1)} %get-tuple-element.14, s32[4096]{0:T(1024)S(1)} %get-tuple-element.15, s32[4096]{0:T(1024)S(1)} %copy-done.2), dimensions={0}, to_apply=%region_0.1 | sort | flops 49152 | bytes 98304 | tf_op jit(solution)/shard_map/sort | solution.py:235
  6.4 0.6 add_select_fusion.order_ref
  7.0 0.6 pad_add_fusion
  7.7 10.8 %shard_map.78 = s32[32,1,256]{2,1,0:T(1,128)} custom-call(s32[32,1,256]{2,1,0:T(1,128)} %bitcast.16), custom_call_target="tpu_custom_call" | custom-call | tf_op jit(solution)/shard_map/pallas_call | solution.py:242
  18.4 0.7 fusion.1
  19.2 6.9 %shard_map.77 = bf16[4096,128]{1,0:T(8,128)(2,1)} custom-call(s32[4096]{0:T(1024)} %add_select_fusion.order_ref, bf16[4096,128]{1,0:T(8,128)(2,1)} %rows_ref.1), custom_call_target="tpu_custom_call" | custom-call | tf_op jit(solution)/shard_map/pallas_call | solution.py:99
  26.1 0.0 copy-start
  26.1 1.2 %copy-done = bf16[4096,128]{1,0:T(8,128)(2,1)S(1)} copy-done((bf16[4096,128]{1,0:T(8,128)(2,1)S(1)}, bf16[4096,128]{1,0:T(8,128)(2,1)}, u32[]{:S(2)}) %copy-start) | copy-done | bytes 1048600
  27.3 58.8 %shard_map.79 = (bf16[32,128,128]{2,1,0:T(8,128)(2,1)S(1)}, s32[8,128]{1,0:T(8,128)S(1)}) custom-call(bf16[32,128,128]{2,1,0:T(8,128)(2,1)S(1)} %bitcast.12, s32[32,128]{1,0:T(8,128)S(1)} %bitcast.15, s32[32,128]{1,0:T(8,128)S(1)} %bitcast.14), custom_call_target="tpu_custom_call" | custom-call | tf_op jit(solution)/shard_map/pallas_call | solution.py:259
  86.1 0.0 copy-start.1
  86.1 1.0 %copy-done.1 = bf16[32,128,128]{2,1,0:T(8,128)(2,1)} copy-done((bf16[32,128,128]{2,1,0:T(8,128)(2,1)}, bf16[32,128,128]{2,1,0:T(8,128)(2,1)S(1)}, u32[]{:S(2)}) %copy-start.1) | copy-done | bytes 1048600
  87.1 0.5 slice.11
  87.6 6.9 %shard_map.80 = bf16[4096,128]{1,0:T(8,128)(2,1)} custom-call(s32[4096]{0:T(1024)} %add_select_fusion.order_ref, bf16[4096,128]{1,0:T(8,128)(2,1)} %bitcast.13), custom_call_target="tpu_custom_call" | custom-call | tf_op jit(solution)/shard_map/pallas_call | solution.py:99
Async XLA Ops:
  0.6 0.8 copy-start.2
  26.1 1.2 %copy-start = (bf16[4096,128]{1,0:T(8,128)(2,1)S(1)}, bf16[4096,128]{1,0:T(8,128)(2,1)}, u32[]{:S(2)}) copy-start(bf16[4096,128]{1,0:T(8,128)(2,1)} %shard_map.77) | copy-start | bytes 3145732
  86.1 1.0 %copy-start.1 = (bf16[32,128,128]{2,1,0:T(8,128)(2,1)}, bf16[32,128,128]{2,1,0:T(8,128)(2,1)S(1)}, u32[]{:S(2)}) copy-start(bf16[32,128,128]{2,1,0:T(8,128)(2,1)S(1)} %get-tuple-element.10) | copy-start | bytes 3145732

commit v2 on v1

--- a/solution.py
+++ b/solution.py
@@ -31,7 +31,7 @@
         return carry
 
     lax.fori_loop(1, devices, greet, 0)
-    pl.semaphore_wait(barrier, devices - 1)
+    return barrier
 
 
 def wait_bytes(ref, sem):
@@ -49,36 +49,6 @@
     ).start()
 
 
-def tags_kernel(devices, narrow_count, tags_ref, got_ref, send_sem, recv_sem):
-    me = my_flat(narrow_count)
-    greet_all(me, devices, narrow_count)
-    pltpu.make_async_copy(tags_ref.at[me], got_ref.at[me], recv_sem).start()
-
-    def send(step, carry):
-        peer = (me + step) % devices
-        send_block(tags_ref.at[peer], got_ref.at[me], send_sem, recv_sem, peer, narrow_count)
-        return carry
-
-    lax.fori_loop(1, devices, send, 0)
-    wait_bytes(got_ref, recv_sem)
-    wait_bytes(tags_ref.at[pl.ds(0, devices - 1)], send_sem)
-
-
-def gather_kernel(unroll, order_ref, rows_ref, out_ref, wide_in, wide_out):
-    count = rows_ref.shape[0]
-    wide_in[...] = rows_ref[...].astype(jnp.float32)
-
-    def move(step, carry):
-        base = pl.multiple_of(step * unroll, unroll)
-        for u in range(unroll):
-            source = order_ref[base + u]
-            wide_out[pl.ds(base + u, 1), :] = wide_in[pl.ds(source, 1), :]
-        return carry
-
-    lax.fori_loop(0, count // unroll, move, 0)
-    out_ref[...] = wide_out[...].astype(out_ref.dtype)
-
-
 def scatter_kernel(unroll, order_ref, rows_ref, out_ref, wide_in, wide_out):
     count = rows_ref.shape[0]
     wide_in[...] = rows_ref[...].astype(jnp.float32)
@@ -94,10 +64,10 @@
     out_ref[...] = wide_out[...].astype(out_ref.dtype)
 
 
-def permute_rows(kernel, order, rows):
+def scatter_rows(order, rows):
     count, cols = rows.shape
     return pl.pallas_call(
-        functools.partial(kernel, 16),
+        functools.partial(scatter_kernel, 16),
         out_shape=jax.ShapeDtypeStruct(rows.shape, rows.dtype),
         in_specs=[pl.BlockSpec(memory_space=SMEM), pl.BlockSpec(memory_space=VMEM)],
         out_specs=pl.BlockSpec(memory_space=VMEM),
@@ -107,37 +77,93 @@
 
 def exchange_kernel(
     devices, narrow_count, chunks, tile,
-    rows_ref, key_one_ref, key_two_ref,
+    order_ref, payload_ref, sent_one, sent_two,
     back_ref, dup_ref,
-    got, totals, means, col_one, col_two, lane_one, wide_rows, dup_mine, dup_all,
+    rows_ref, wide_in, wide_slot, got_one, got_two,
+    got, totals, means, col_one, col_two, lane_one, lane_two, wide_rows, dup_mine, dup_all,
+    tag_send, tag_recv,
     send_sem, recv_sems, back_send, back_recv, dup_send, dup_recv,
 ):
     _, slot_rows, cols = rows_ref.shape
     count = devices * slot_rows
     chunk_slots = devices // chunks
     chunk_rows = chunk_slots * slot_rows
-    lanes = key_one_ref.shape[1]
+    lanes = lane_one.shape[1]
     me = my_flat(narrow_count)
     my_chunk = me // chunk_slots
-    greet_all(me, devices, narrow_count)
-
+    barrier = greet_all(me, devices, narrow_count)
+    wide_in[...] = payload_ref[...].astype(jnp.float32)
+    pl.semaphore_wait(barrier, devices - 1)
+
+    pltpu.make_async_copy(sent_one.at[me], got_one.at[me], tag_recv.at[0]).start()
+    pltpu.make_async_copy(sent_two.at[me], got_two.at[me], tag_recv.at[1]).start()
+
+    def send_tags(step, carry):
+        peer = (me + step) % devices
+        send_block(
+            sent_one.at[peer], got_one.at[me], tag_send.at[0], tag_recv.at[0], peer, narrow_count
+        )
+        send_block(
+            sent_two.at[peer], got_two.at[me], tag_send.at[1], tag_recv.at[1], peer, narrow_count
+        )
+        return carry
+
+    lax.fori_loop(1, devices, send_tags, 0)
+
+    def peer_of(step):
+        chunk = step // chunk_slots
+        first = ((my_chunk + chunk) % chunks) * chunk_slots
+        return chunk, first + (me + step) % chunk_slots
+
+    def send_slot(step):
+        chunk, peer = peer_of(step)
+        send_block(
+            rows_ref.at[peer], got.at[me], send_sem, recv_sems.at[chunk], peer, narrow_count
+        )
+
+    unroll = min(16, slot_rows)
+
+    def fill(step, carry):
+        _, peer = peer_of(step)
+
+        def move(inner, carry):
+            base = pl.multiple_of(inner * unroll, unroll)
+            for u in range(unroll):
+                source = order_ref[peer * slot_rows + base + u]
+                wide_slot[pl.ds(base + u, 1), :] = wide_in[pl.ds(source, 1), :]
+            return carry
+
+        lax.fori_loop(0, slot_rows // unroll, move, 0)
+        rows_ref[peer] = wide_slot[...].astype(rows_ref.dtype)
+
+        @pl.when(step > 1)
+        def _():
+            send_slot(step - 1)
+
+        return carry
+
+    lax.fori_loop(0, devices, fill, 0)
     pltpu.make_async_copy(rows_ref.at[me], got.at[me], recv_sems.at[0]).start()
-    for c in range(chunks):
-        first = ((my_chunk + c) % chunks) * chunk_slots
-
-        def send(step, carry, first=first, c=c):
-            peer = first + (me + step) % chunk_slots
-            send_block(
-                rows_ref.at[peer], got.at[me], send_sem, recv_sems.at[c], peer, narrow_count
-            )
-            return carry
-
-        lax.fori_loop(1 if c == 0 else 0, chunk_slots, send, 0)
-
-    one = key_one_ref[...]
+
+    wait_bytes(got_one, tag_recv.at[0])
+    send_slot(devices - 1)
+    wait_bytes(got_two, tag_recv.at[1])
+    if slot_rows >= lanes:
+        per_slot = slot_rows // lanes
+        for r in range(count // lanes):
+            piece = pl.ds(r % per_slot * lanes, lanes)
+            lane_one[r : r + 1, :] = got_one[r // per_slot, :, piece]
+            lane_two[r : r + 1, :] = got_two[r // per_slot, :, piece]
+    else:
+        group = lanes // slot_rows
+        for r in range(count // lanes):
+            pieces = range(r * group, (r + 1) * group)
+            lane_one[r : r + 1, :] = jnp.concatenate([got_one[p] for p in pieces], axis=1)
+            lane_two[r : r + 1, :] = jnp.concatenate([got_two[p] for p in pieces], axis=1)
+    one = lane_one[...]
+    flipped_one = one.T
+    flipped_two = lane_two[...].T
     lane_one[...] = jnp.where(one < 0, -2, one)
-    flipped_one = one.T
-    flipped_two = key_two_ref[...].T
     for r in range(count // lanes):
         at = pl.ds(r * lanes, lanes)
         col_one[at, :] = jnp.broadcast_to(flipped_one[:, r : r + 1], (lanes, lanes))
@@ -177,7 +203,7 @@
             parts = []
             for b in range(chunk_rows // lanes):
                 row_at = pl.ds(lane_base + b, 1)
-                same = (left_one == lane_one[row_at, :]) & (left_two == key_two_ref[row_at, :])
+                same = (left_one == lane_one[row_at, :]) & (left_two == lane_two[row_at, :])
                 parts.append(jnp.where(same, 1.0, 0.0).astype(jnp.bfloat16))
             mask = jnp.concatenate(parts, axis=1)
             part = jnp.dot(mask, wide_rows[...], preferred_element_type=jnp.float32)
@@ -219,6 +245,8 @@
     wait_bytes(dup_all, dup_recv)
     dup_ref[...] = jnp.sum(dup_all[...], axis=0).astype(jnp.int32)
     wait_bytes(back_ref, back_recv)
+    wait_bytes(sent_one.at[pl.ds(0, devices - 1)], tag_send.at[0])
+    wait_bytes(sent_two.at[pl.ds(0, devices - 1)], tag_send.at[1])
     wait_bytes(rows_ref.at[pl.ds(0, devices - 1)], send_sem)
     wait_bytes(means.at[pl.ds(0, devices - 1)], back_send)
     wait_bytes(dup_all.at[pl.ds(0, devices - 1)], dup_send)
@@ -236,22 +264,8 @@
         (packed, jnp.where(live > 0, first_key, -1), second_key), num_keys=1, is_stable=False
     )
     order = packed % row_count
-    tags = jnp.stack(
-        [key_one.reshape(devices, slot_rows), key_two.reshape(devices, slot_rows)], axis=1
-    ).reshape(devices, 1, 2 * slot_rows)
-    got_tags = pl.pallas_call(
-        functools.partial(tags_kernel, devices, narrow_count),
-        out_shape=jax.ShapeDtypeStruct(tags.shape, tags.dtype),
-        in_specs=[pl.BlockSpec(memory_space=VMEM)],
-        out_specs=pl.BlockSpec(memory_space=VMEM),
-        scratch_shapes=[pltpu.SemaphoreType.DMA, pltpu.SemaphoreType.DMA],
-        compiler_params=pltpu.CompilerParams(collective_id=0, has_side_effects=True),
-    )(tags)
     lanes = 128
-    keys_one = got_tags[:, 0, :slot_rows].reshape(row_count // lanes, lanes)
-    keys_two = got_tags[:, 0, slot_rows:].reshape(row_count // lanes, lanes)
-    sent = permute_rows(gather_kernel, order, payload).reshape(devices, slot_rows, cols)
-
+    tags = (devices, 1, slot_rows)
     chunks = 4 if devices % 4 == 0 else 1
     tile = max(256, slot_rows)
     tile = min(tile, row_count)
@@ -262,18 +276,26 @@
             jax.ShapeDtypeStruct(block, payload.dtype),
             jax.ShapeDtypeStruct((8, cols), jnp.int32),
         ),
-        in_specs=[pl.BlockSpec(memory_space=VMEM)] * 3,
+        in_specs=[pl.BlockSpec(memory_space=SMEM)] + [pl.BlockSpec(memory_space=VMEM)] * 3,
         out_specs=(pl.BlockSpec(memory_space=VMEM), pl.BlockSpec(memory_space=VMEM)),
         scratch_shapes=[
+            VMEM(block, payload.dtype),
+            VMEM((row_count, cols), jnp.float32),
+            VMEM((slot_rows, cols), jnp.float32),
+            VMEM(tags, jnp.int32),
+            VMEM(tags, jnp.int32),
             VMEM(block, payload.dtype),
             VMEM((row_count, 2 * cols), jnp.float32),
             VMEM(block, payload.dtype),
             VMEM((row_count, lanes), jnp.int32),
             VMEM((row_count, lanes), jnp.int32),
             VMEM((row_count // lanes, lanes), jnp.int32),
+            VMEM((row_count // lanes, lanes), jnp.int32),
             VMEM((row_count // chunks, 2 * cols), payload.dtype),
             VMEM((2, 8, cols), jnp.float32),
             VMEM((devices, 8, cols), jnp.float32),
+            pltpu.SemaphoreType.DMA((2,)),
+            pltpu.SemaphoreType.DMA((2,)),
             pltpu.SemaphoreType.DMA,
             pltpu.SemaphoreType.DMA((chunks,)),
             pltpu.SemaphoreType.DMA,
@@ -282,10 +304,10 @@
             pltpu.SemaphoreType.DMA,
         ],
         compiler_params=pltpu.CompilerParams(
-            collective_id=1, has_side_effects=True, vmem_limit_bytes=48 * 1024 * 1024
+            collective_id=0, has_side_effects=True, vmem_limit_bytes=48 * 1024 * 1024
         ),
-    )(sent, keys_one, keys_two)
-    group_mean = permute_rows(scatter_kernel, order, back.reshape(row_count, cols))
+    )(order, payload, key_one.reshape(tags), key_two.reshape(tags))
+    group_mean = scatter_rows(order, back.reshape(row_count, cols))
     return (group_mean, dups[0, 0])
 
 

time: 95 us -> 79.7 us (0.84)
  Pallas kernels: 83.3 us -> 70.1 us
  other arithmetic: 7.02 us -> 5.78 us
    pallas_call x3 -> x1, Pallas kernels: 24.5 us -> 6.89 us  [scatter_rows(): pl.pallas_call(functools.partial(scatter_kernel, 16), out_shape=jax.Shape...]
    pallas_call x1, Pallas kernels: 58.8 us -> 63.2 us  [on_device(): pl.pallas_call(functools.partial(exchange_kernel, devices, narrow_count,...]
    unnamed x6 -> x8, local copies, waits for them, and re-layouts: 2.21 us -> 2.21 us
where the time goes in v2:
time: 79.7 us; the launch traced here: 79.3 us
  Pallas kernels  70.1 us (88%)
  other arithmetic  5.78 us (7%)
  local copies, waits for them, and re-layouts  2.72 us (3%)
    pallas_call x1, Pallas kernels, on_device(): pl.pallas_call(functools.partial(exchange_kernel, devices, narrow_count,...  63.2 us
    pallas_call x1, Pallas kernels, scatter_rows(): pl.pallas_call(functools.partial(scatter_kernel, 16), out_shape=jax.Shape...  6.89 us
    sort x1, other arithmetic, on_device(): lax.sort((packed, jnp.where(live > 0, first_key, -1), second_key), num_ke...  4.98 us
    unnamed x8, local copies, waits for them, and re-layouts  2.21 us

profile of v2, /device:TPU:0, one launch (start us, length us, event | category | flops | bytes accessed | tf_op | source)
XLA Modules:
  0.0 79.3 jit_solution(5025571302093555153)
XLA Ops:
  0.6 0.0 copy-start.3
  0.6 0.8 iota_add_fusion
  1.4 0.0 copy-done.3
  1.4 5.0 %sort.21 = (s32[4096]{0:T(1024)S(1)}, s32[4096]{0:T(1024)S(1)}, s32[4096]{0:T(1024)S(1)}) sort(s32[4096]{0:T(1024)S(1)} %get-tuple-element.12, s32[4096]{0:T(1024)S(1)} %get-tuple-element.13, s32[4096]{0:T(1024)S(1)} %copy-done.3), dimensions={0}, to_apply=%region_0.1 | sort | flops 49152 | bytes 98304 | tf_op jit(solution)/shard_map/sort | solution.py:263
  6.4 0.0 copy-start.2
  6.4 0.0 copy-start
  6.5 1.2 %copy-done = bf16[4096,128]{1,0:T(8,128)(2,1)S(1)} copy-done((bf16[4096,128]{1,0:T(8,128)(2,1)S(1)}, bf16[4096,128]{1,0:T(8,128)(2,1)}, u32[]{:S(2)}) %copy-start) | copy-done | bytes 1048600
  7.7 63.2 %shard_map.77 = (bf16[32,128,128]{2,1,0:T(8,128)(2,1)S(1)}, s32[8,128]{1,0:T(8,128)S(1)}) custom-call(s32[4096]{0:T(1024)S(1)} %add_select_fusion.order_ref, bf16[4096,128]{1,0:T(8,128)(2,1)S(1)} %copy-done, s32[32,1,128]{2,1,0:T(1,128)S(1)} %bitcast.5, s32[32,1,128]{2,1,0:T(1,128)S(1)} %bitcast.6), custom_call_target="tpu_custom_call" | custom-call | tf_op jit(solution)/shard_map/pallas_call | solution.py:273
  70.9 0.0 copy-done.2
  70.9 0.0 copy-start.1
  70.9 1.0 %copy-done.1 = bf16[32,128,128]{2,1,0:T(8,128)(2,1)} copy-done((bf16[32,128,128]{2,1,0:T(8,128)(2,1)}, bf16[32,128,128]{2,1,0:T(8,128)(2,1)S(1)}, u32[]{:S(2)}) %copy-start.1) | copy-done | bytes 1048600
  71.9 0.5 slice.3
  72.4 6.9 %shard_map.78 = bf16[4096,128]{1,0:T(8,128)(2,1)} custom-call(s32[4096]{0:T(1024)} %copy-done.2, bf16[4096,128]{1,0:T(8,128)(2,1)} %bitcast.4), custom_call_target="tpu_custom_call" | custom-call | tf_op jit(solution)/shard_map/pallas_call | solution.py:69
  (1 shorter events, 0.0 us)
Async XLA Ops:
  0.6 0.8 %copy-start.3 = (s32[4096]{0:T(1024)S(1)}, s32[4096]{0:T(1024)}, u32[]{:S(2)}) copy-start(s32[4096]{0:T(1024)} %param.8) | copy-start | bytes 49156
  6.4 64.5 %copy-start.2 = (s32[4096]{0:T(1024)}, s32[4096]{0:T(1024)S(1)}, u32[]{:S(2)}) copy-start(s32[4096]{0:T(1024)S(1)} %add_select_fusion.order_ref) | copy-start | bytes 49156
  6.4 1.2 %copy-start = (bf16[4096,128]{1,0:T(8,128)(2,1)S(1)}, bf16[4096,128]{1,0:T(8,128)(2,1)}, u32[]{:S(2)}) copy-start(bf16[4096,128]{1,0:T(8,128)(2,1)} %payload_ref.1) | copy-start | bytes 3145732
  70.9 1.0 %copy-start.1 = (bf16[32,128,128]{2,1,0:T(8,128)(2,1)}, bf16[32,128,128]{2,1,0:T(8,128)(2,1)S(1)}, u32[]{:S(2)}) copy-start(bf16[32,128,128]{2,1,0:T(8,128)(2,1)S(1)} %get-tuple-element.10) | copy-start | bytes 3145732

commit v3 on v2

--- a/solution.py
+++ b/solution.py
@@ -49,9 +49,19 @@
     ).start()
 
 
-def scatter_kernel(unroll, order_ref, rows_ref, out_ref, wide_in, wide_out):
-    count = rows_ref.shape[0]
-    wide_in[...] = rows_ref[...].astype(jnp.float32)
+def scatter_kernel(unroll, parts, order_ref, dups_ref, rows_any, out_ref, dup_ref,
+                   rows_in, wide_in, wide_out, sems):
+    count = rows_in.shape[0]
+    part = count // parts
+    copies = [
+        pltpu.make_async_copy(
+            rows_any.at[pl.ds(p * part, part)], rows_in.at[pl.ds(p * part, part)], sems.at[p]
+        )
+        for p in range(parts)
+    ]
+    for copy in copies:
+        copy.start()
+    dup_ref[0] = dups_ref[0, 0]
 
     def move(step, carry):
         base = pl.multiple_of(step * unroll, unroll)
@@ -60,28 +70,46 @@
             wide_out[pl.ds(target, 1), :] = wide_in[pl.ds(base + u, 1), :]
         return carry
 
-    lax.fori_loop(0, count // unroll, move, 0)
+    for p, copy in enumerate(copies):
+        copy.wait()
+        at = pl.ds(p * part, part)
+        wide_in[at, :] = rows_in[at, :].astype(jnp.float32)
+        lax.fori_loop(p * part // unroll, (p + 1) * part // unroll, move, 0)
     out_ref[...] = wide_out[...].astype(out_ref.dtype)
 
 
-def scatter_rows(order, rows):
+def scatter_rows(order, dups, rows):
     count, cols = rows.shape
+    parts = 4
     return pl.pallas_call(
-        functools.partial(scatter_kernel, 16),
-        out_shape=jax.ShapeDtypeStruct(rows.shape, rows.dtype),
-        in_specs=[pl.BlockSpec(memory_space=SMEM), pl.BlockSpec(memory_space=VMEM)],
-        out_specs=pl.BlockSpec(memory_space=VMEM),
-        scratch_shapes=[VMEM((count, cols), jnp.float32), VMEM((count, cols), jnp.float32)],
-    )(order, rows)
+        functools.partial(scatter_kernel, 16, parts),
+        out_shape=(
+            jax.ShapeDtypeStruct(rows.shape, rows.dtype),
+            jax.ShapeDtypeStruct((1,), jnp.int32),
+        ),
+        in_specs=[
+            pl.BlockSpec(memory_space=SMEM),
+            pl.BlockSpec(memory_space=VMEM),
+            pl.BlockSpec(memory_space=pl.ANY),
+        ],
+        out_specs=(pl.BlockSpec(memory_space=VMEM), pl.BlockSpec(memory_space=SMEM)),
+        scratch_shapes=[
+            VMEM((count, cols), rows.dtype),
+            VMEM((count, cols), jnp.float32),
+            VMEM((count, cols), jnp.float32),
+            pltpu.SemaphoreType.DMA((parts,)),
+        ],
+        compiler_params=pltpu.CompilerParams(vmem_limit_bytes=16 * 1024 * 1024),
+    )(order, dups, rows)
 
 
 def exchange_kernel(
     devices, narrow_count, chunks, tile,
-    order_ref, payload_ref, sent_one, sent_two,
+    order_ref, payload_any, sent_one, sent_two,
     back_ref, dup_ref,
     rows_ref, wide_in, wide_slot, got_one, got_two,
     got, totals, means, col_one, col_two, lane_one, lane_two, wide_rows, dup_mine, dup_all,
-    tag_send, tag_recv,
+    payload_ref, load_sem, tag_send, tag_recv,
     send_sem, recv_sems, back_send, back_recv, dup_send, dup_recv,
 ):
     _, slot_rows, cols = rows_ref.shape
@@ -91,7 +119,10 @@
     lanes = lane_one.shape[1]
     me = my_flat(narrow_count)
     my_chunk = me // chunk_slots
+    load = pltpu.make_async_copy(payload_any, payload_ref, load_sem)
+    load.start()
     barrier = greet_all(me, devices, narrow_count)
+    load.wait()
     wide_in[...] = payload_ref[...].astype(jnp.float32)
     pl.semaphore_wait(barrier, devices - 1)
 
@@ -112,8 +143,8 @@
 
     def peer_of(step):
         chunk = step // chunk_slots
-        first = ((my_chunk + chunk) % chunks) * chunk_slots
-        return chunk, first + (me + step) % chunk_slots
+        first = ((my_chunk + 1 + chunk) % chunks) * chunk_slots
+        return chunk, first + (me + 1 + step) % chunk_slots
 
     def send_slot(step):
         chunk, peer = peer_of(step)
@@ -136,17 +167,16 @@
         lax.fori_loop(0, slot_rows // unroll, move, 0)
         rows_ref[peer] = wide_slot[...].astype(rows_ref.dtype)
 
-        @pl.when(step > 1)
+        @pl.when(step > 0)
         def _():
             send_slot(step - 1)
 
         return carry
 
     lax.fori_loop(0, devices, fill, 0)
-    pltpu.make_async_copy(rows_ref.at[me], got.at[me], recv_sems.at[0]).start()
+    pltpu.make_async_copy(rows_ref.at[me], got.at[me], recv_sems.at[chunks - 1]).start()
 
     wait_bytes(got_one, tag_recv.at[0])
-    send_slot(devices - 1)
     wait_bytes(got_two, tag_recv.at[1])
     if slot_rows >= lanes:
         per_slot = slot_rows // lanes
@@ -173,7 +203,7 @@
 
     tiles = count // tile
     tile_slots = tile // slot_rows
-    my_tile = me // tile_slots
+    lead = me // tile_slots + max(1, tiles // chunks)
 
     def send_tile(index):
         for u in range(tile_slots):
@@ -189,14 +219,17 @@
                     means.at[peer], back_ref.at[me], back_send, back_recv, peer, narrow_count
                 )
 
-    for c in range(chunks):
-        first = ((my_chunk - c + chunks) % chunks) * chunk_slots
+    turns = list(range(chunks))
+    if chunks > 2:
+        turns = turns[: chunks - 2] + [chunks - 1, chunks - 2]
+    for turn, c in enumerate(turns):
+        first = ((my_chunk - 1 - c + 2 * chunks) % chunks) * chunk_slots
         wait_bytes(got.at[pl.ds(first, chunk_slots)], recv_sems.at[c])
         wide_rows[:, :cols] = got[pl.ds(first, chunk_slots)].reshape(chunk_rows, cols)
         lane_base = first * slot_rows // lanes
 
-        def body(step, carry, c=c, lane_base=lane_base):
-            index = (my_tile + step) % tiles
+        def body(step, carry, turn=turn, lane_base=lane_base):
+            index = (lead + step) % tiles
             at = pl.ds(pl.multiple_of(index * tile, tile), tile)
             left_one = col_one[at, :]
             left_two = col_two[at, :]
@@ -207,9 +240,9 @@
                 parts.append(jnp.where(same, 1.0, 0.0).astype(jnp.bfloat16))
             mask = jnp.concatenate(parts, axis=1)
             part = jnp.dot(mask, wide_rows[...], preferred_element_type=jnp.float32)
-            if c > 0:
+            if turn > 0:
                 part = part + totals[at, :]
-            if c < chunks - 1:
+            if turn < chunks - 1:
                 totals[at, :] = part
             else:
                 sums = part[:, :cols]
@@ -225,7 +258,7 @@
 
                 @pl.when(step > 0)
                 def _():
-                    send_tile((my_tile + step + tiles - 1) % tiles)
+                    send_tile((lead + step + tiles - 1) % tiles)
             return carry
 
         lax.fori_loop(0, tiles, body, 0)
@@ -233,7 +266,7 @@
     live_rows = jnp.sum(dup_mine[0], axis=0, keepdims=True)
     groups = jnp.floor(jnp.sum(dup_mine[1], axis=0, keepdims=True) + 0.5)
     dup_mine[0] = jnp.broadcast_to(live_rows - groups, (8, cols))
-    send_tile((my_tile + tiles - 1) % tiles)
+    send_tile((lead + tiles - 1) % tiles)
     pltpu.make_async_copy(dup_mine.at[0], dup_all.at[me], dup_recv).start()
 
     def send_dup(step, carry):
@@ -276,7 +309,12 @@
             jax.ShapeDtypeStruct(block, payload.dtype),
             jax.ShapeDtypeStruct((8, cols), jnp.int32),
         ),
-        in_specs=[pl.BlockSpec(memory_space=SMEM)] + [pl.BlockSpec(memory_space=VMEM)] * 3,
+        in_specs=[
+            pl.BlockSpec(memory_space=SMEM),
+            pl.BlockSpec(memory_space=pltpu.HBM),
+            pl.BlockSpec(memory_space=VMEM),
+            pl.BlockSpec(memory_space=VMEM),
+        ],
         out_specs=(pl.BlockSpec(memory_space=VMEM), pl.BlockSpec(memory_space=VMEM)),
         scratch_shapes=[
             VMEM(block, payload.dtype),
@@ -294,6 +332,8 @@
             VMEM((row_count // chunks, 2 * cols), payload.dtype),
             VMEM((2, 8, cols), jnp.float32),
             VMEM((devices, 8, cols), jnp.float32),
+            VMEM((row_count, cols), payload.dtype),
+            pltpu.SemaphoreType.DMA,
             pltpu.SemaphoreType.DMA((2,)),
             pltpu.SemaphoreType.DMA((2,)),
             pltpu.SemaphoreType.DMA,
@@ -307,8 +347,8 @@
             collective_id=0, has_side_effects=True, vmem_limit_bytes=48 * 1024 * 1024
         ),
     )(order, payload, key_one.reshape(tags), key_two.reshape(tags))
-    group_mean = scatter_rows(order, back.reshape(row_count, cols))
-    return (group_mean, dups[0, 0])
+    group_mean, total = scatter_rows(order, dups, back.reshape(row_count, cols))
+    return (group_mean, total[0])
 
 
 def solution(mesh):

time: 79.7 us -> 80.5 us (1.010)
  Pallas kernels: 70.1 us -> 72.6 us
  local copies, waits for them, and re-layouts: 2.72 us -> 1.22 us
    pallas_call x1, Pallas kernels: 63.2 us -> 66 us  [on_device(): pl.pallas_call(functools.partial(exchange_kernel, devices, narrow_count,...]
    unnamed x8 -> x4, local copies, waits for them, and re-layouts: 2.21 us -> 1.22 us
where the time goes in v3:
time: 80.5 us; the launch traced here: 80.2 us
  Pallas kernels  72.6 us (90%)
  other arithmetic  5.78 us (7%)
  local copies, waits for them, and re-layouts  1.22 us (2%)
    pallas_call x1, Pallas kernels, on_device(): pl.pallas_call(functools.partial(exchange_kernel, devices, narrow_count,...  66 us
    pallas_call x1, Pallas kernels, scatter_rows(): pl.pallas_call(functools.partial(scatter_kernel, 16, parts), out_shape=(j...  6.51 us
    sort x1, other arithmetic, on_device(): lax.sort((packed, jnp.where(live > 0, first_key, -1), second_key), num_ke...  4.98 us

profile of v3, /device:TPU:0, one launch (start us, length us, event | category | flops | bytes accessed | tf_op | source)
XLA Modules:
  0.0 80.2 jit_solution(459478189416396490)
XLA Ops:
  0.6 0.0 copy-start.1
  0.6 0.8 iota_add_fusion
  1.4 0.0 copy-done.1
  1.4 5.0 %sort.21 = (s32[4096]{0:T(1024)S(1)}, s32[4096]{0:T(1024)S(1)}, s32[4096]{0:T(1024)S(1)}) sort(s32[4096]{0:T(1024)S(1)} %get-tuple-element.16, s32[4096]{0:T(1024)S(1)} %get-tuple-element.17, s32[4096]{0:T(1024)S(1)} %copy-done.1), dimensions={0}, to_apply=%region_0.1 | sort | flops 49152 | bytes 98304 | tf_op jit(solution)/shard_map/sort | solution.py:296
  6.4 0.0 copy-start
  6.4 1.2 %copy-done = bf16[4096,128]{1,0:T(8,128)(2,1)S(1)} copy-done((bf16[4096,128]{1,0:T(8,128)(2,1)S(1)}, bf16[4096,128]{1,0:T(8,128)(2,1)}, u32[]{:S(2)}) %copy-start) | copy-done | bytes 1048600
  7.7 66.0 %shard_map.77 = (bf16[32,128,128]{2,1,0:T(8,128)(2,1)S(1)}, s32[8,128]{1,0:T(8,128)S(1)}) custom-call(s32[4096]{0:T(1024)S(1)} %add_select_fusion.order_ref, bf16[4096,128]{1,0:T(8,128)(2,1)S(1)} %copy-done, s32[32,1,128]{2,1,0:T(1,128)S(1)} %bitcast.5, s32[32,1,128]{2,1,0:T(1,128)S(1)} %bitcast.6), custom_call_target="tpu_custom_call" | custom-call | tf_op jit(solution)/shard_map/pallas_call | solution.py:306
  73.7 6.5 %shard_map.78 = (bf16[4096,128]{1,0:T(8,128)(2,1)}, s32[1]{0:T(128)}) custom-call(s32[4096]{0:T(1024)S(1)} %add_select_fusion.order_ref, s32[8,128]{1,0:T(8,128)S(1)} %get-tuple-element.12.dups_ref, bf16[4096,128]{1,0:T(8,128)(2,1)S(1)} %bitcast.4), custom_call_target="tpu_custom_call" | custom-call | tf_op jit(solution)/shard_map/pallas_call | solution.py:84
  (1 shorter events, 0.0 us)
Async XLA Ops:
  0.6 0.8 copy-start.1
  6.4 1.2 %copy-start = (bf16[4096,128]{1,0:T(8,128)(2,1)S(1)}, bf16[4096,128]{1,0:T(8,128)(2,1)}, u32[]{:S(2)}) copy-start(bf16[4096,128]{1,0:T(8,128)(2,1)} %payload_any.1) | copy-start | bytes 3145732

commit v4 on v3

--- a/solution.py
+++ b/solution.py
@@ -104,7 +104,7 @@
 
 
 def exchange_kernel(
-    devices, narrow_count, chunks, tile,
+    devices, narrow_count, chunks, groups, tile,
     order_ref, payload_any, sent_one, sent_two,
     back_ref, dup_ref,
     rows_ref, wide_in, wide_slot, got_one, got_two,
@@ -115,10 +115,15 @@
     _, slot_rows, cols = rows_ref.shape
     count = devices * slot_rows
     chunk_slots = devices // chunks
-    chunk_rows = chunk_slots * slot_rows
     lanes = lane_one.shape[1]
     me = my_flat(narrow_count)
     my_chunk = me // chunk_slots
+    unit_slots = max(1, lanes // slot_rows)
+    unit_rows = unit_slots * slot_rows
+    units = chunk_slots // unit_slots
+    group_units = units // groups
+    group_slots = devices // groups
+    my_unit = me % chunk_slots // unit_slots
     load = pltpu.make_async_copy(payload_any, payload_ref, load_sem)
     load.start()
     barrier = greet_all(me, devices, narrow_count)
@@ -142,14 +147,17 @@
     lax.fori_loop(1, devices, send_tags, 0)
 
     def peer_of(step):
-        chunk = step // chunk_slots
-        first = ((my_chunk + 1 + chunk) % chunks) * chunk_slots
-        return chunk, first + (me + 1 + step) % chunk_slots
+        rest = step % group_slots
+        turn = rest // chunks
+        first = (my_chunk + rest % chunks) % chunks * chunk_slots
+        offset = step // group_slots * group_units + turn // unit_slots
+        unit = (my_unit + offset) % units
+        return step // group_slots, first + unit * unit_slots + (me + turn) % unit_slots
 
     def send_slot(step):
-        chunk, peer = peer_of(step)
+        group, peer = peer_of(step)
         send_block(
-            rows_ref.at[peer], got.at[me], send_sem, recv_sems.at[chunk], peer, narrow_count
+            rows_ref.at[peer], got.at[me], send_sem, recv_sems.at[group], peer, narrow_count
         )
 
     unroll = min(16, slot_rows)
@@ -167,16 +175,17 @@
         lax.fori_loop(0, slot_rows // unroll, move, 0)
         rows_ref[peer] = wide_slot[...].astype(rows_ref.dtype)
 
-        @pl.when(step > 0)
+        @pl.when(step > 1)
         def _():
             send_slot(step - 1)
 
         return carry
 
     lax.fori_loop(0, devices, fill, 0)
-    pltpu.make_async_copy(rows_ref.at[me], got.at[me], recv_sems.at[chunks - 1]).start()
+    pltpu.make_async_copy(rows_ref.at[me], got.at[me], recv_sems.at[0]).start()
 
     wait_bytes(got_one, tag_recv.at[0])
+    send_slot(devices - 1)
     wait_bytes(got_two, tag_recv.at[1])
     if slot_rows >= lanes:
         per_slot = slot_rows // lanes
@@ -198,12 +207,11 @@
         at = pl.ds(r * lanes, lanes)
         col_one[at, :] = jnp.broadcast_to(flipped_one[:, r : r + 1], (lanes, lanes))
         col_two[at, :] = jnp.broadcast_to(flipped_two[:, r : r + 1], (lanes, lanes))
-    wide_rows[:, cols:] = jnp.ones((chunk_rows, cols), wide_rows.dtype)
+    wide_rows[:, cols:] = jnp.ones((group_slots * slot_rows, cols), wide_rows.dtype)
     dup_mine[...] = jnp.zeros_like(dup_mine)
 
     tiles = count // tile
     tile_slots = tile // slot_rows
-    lead = me // tile_slots + max(1, tiles // chunks)
 
     def send_tile(index):
         for u in range(tile_slots):
@@ -219,30 +227,39 @@
                     means.at[peer], back_ref.at[me], back_send, back_recv, peer, narrow_count
                 )
 
-    turns = list(range(chunks))
-    if chunks > 2:
-        turns = turns[: chunks - 2] + [chunks - 1, chunks - 2]
-    for turn, c in enumerate(turns):
-        first = ((my_chunk - 1 - c + 2 * chunks) % chunks) * chunk_slots
-        wait_bytes(got.at[pl.ds(first, chunk_slots)], recv_sems.at[c])
-        wide_rows[:, :cols] = got[pl.ds(first, chunk_slots)].reshape(chunk_rows, cols)
-        lane_base = first * slot_rows // lanes
-
-        def body(step, carry, turn=turn, lane_base=lane_base):
-            index = (lead + step) % tiles
+    plane_tiles = tiles // chunks
+
+    def tile_of(step):
+        plane = (my_chunk + step) % chunks
+        return plane * plane_tiles + (me + step // chunks) % plane_tiles
+
+    for g in range(groups):
+        wait_bytes(got.at[pl.ds(0, group_slots)], recv_sems.at[g])
+        lane_bases = []
+        for c in range(chunks):
+            for o in range(group_units):
+                unit = (my_unit - g * group_units - o + 2 * units) % units
+                first = (my_chunk + c) % chunks * chunk_slots + unit * unit_slots
+                to = pl.ds(len(lane_bases) * unit_rows, unit_rows)
+                wide_rows[to, :cols] = got[pl.ds(first, unit_slots)].reshape(unit_rows, cols)
+                lane_bases.append(first * slot_rows // lanes)
+
+        def body(step, carry, g=g, lane_bases=tuple(lane_bases)):
+            index = tile_of(step)
             at = pl.ds(pl.multiple_of(index * tile, tile), tile)
             left_one = col_one[at, :]
             left_two = col_two[at, :]
             parts = []
-            for b in range(chunk_rows // lanes):
-                row_at = pl.ds(lane_base + b, 1)
+            for b in range(group_slots * slot_rows // lanes):
+                per_unit = unit_rows // lanes
+                row_at = pl.ds(lane_bases[b // per_unit] + b % per_unit, 1)
                 same = (left_one == lane_one[row_at, :]) & (left_two == lane_two[row_at, :])
                 parts.append(jnp.where(same, 1.0, 0.0).astype(jnp.bfloat16))
             mask = jnp.concatenate(parts, axis=1)
             part = jnp.dot(mask, wide_rows[...], preferred_element_type=jnp.float32)
-            if turn > 0:
+            if g > 0:
                 part = part + totals[at, :]
-            if turn < chunks - 1:
+            if g < groups - 1:
                 totals[at, :] = part
             else:
                 sums = part[:, :cols]
@@ -258,7 +275,7 @@
 
                 @pl.when(step > 0)
                 def _():
-                    send_tile((lead + step + tiles - 1) % tiles)
+                    send_tile(tile_of(step - 1))
             return carry
 
         lax.fori_loop(0, tiles, body, 0)
@@ -266,7 +283,7 @@
     live_rows = jnp.sum(dup_mine[0], axis=0, keepdims=True)
     groups = jnp.floor(jnp.sum(dup_mine[1], axis=0, keepdims=True) + 0.5)
     dup_mine[0] = jnp.broadcast_to(live_rows - groups, (8, cols))
-    send_tile((lead + tiles - 1) % tiles)
+    send_tile(tile_of(tiles - 1))
     pltpu.make_async_copy(dup_mine.at[0], dup_all.at[me], dup_recv).start()
 
     def send_dup(step, carry):
@@ -299,12 +316,14 @@
     order = packed % row_count
     lanes = 128
     tags = (devices, 1, slot_rows)
-    chunks = 4 if devices % 4 == 0 else 1
+    unit_slots = max(1, lanes // slot_rows)
+    chunks = 4 if devices % (4 * unit_slots) == 0 else 1
+    groups = 4 if devices % (4 * chunks * unit_slots) == 0 else 1
     tile = max(256, slot_rows)
     tile = min(tile, row_count)
     block = (devices, slot_rows, cols)
     back, dups = pl.pallas_call(
-        functools.partial(exchange_kernel, devices, narrow_count, chunks, tile),
+        functools.partial(exchange_kernel, devices, narrow_count, chunks, groups, tile),
         out_shape=(
             jax.ShapeDtypeStruct(block, payload.dtype),
             jax.ShapeDtypeStruct((8, cols), jnp.int32),
@@ -329,7 +348,7 @@
             VMEM((row_count, lanes), jnp.int32),
             VMEM((row_count // lanes, lanes), jnp.int32),
             VMEM((row_count // lanes, lanes), jnp.int32),
-            VMEM((row_count // chunks, 2 * cols), payload.dtype),
+            VMEM((row_count // groups, 2 * cols), payload.dtype),
             VMEM((2, 8, cols), jnp.float32),
             VMEM((devices, 8, cols), jnp.float32),
             VMEM((row_count, cols), payload.dtype),
@@ -337,7 +356,7 @@
             pltpu.SemaphoreType.DMA((2,)),
             pltpu.SemaphoreType.DMA((2,)),
             pltpu.SemaphoreType.DMA,
-            pltpu.SemaphoreType.DMA((chunks,)),
+            pltpu.SemaphoreType.DMA((groups,)),
             pltpu.SemaphoreType.DMA,
             pltpu.SemaphoreType.DMA,
             pltpu.SemaphoreType.DMA,

time: 80.5 us -> 79.6 us (0.989)
  Pallas kernels: 72.6 us -> 71.6 us
    pallas_call x1, Pallas kernels: 66 us -> 65.1 us  [on_device(): pl.pallas_call(functools.partial(exchange_kernel, devices, narrow_count,...]
where the time goes in v4:
time: 79.6 us; the launch traced here: 79.3 us
  Pallas kernels  71.6 us (90%)
  other arithmetic  5.78 us (7%)
  local copies, waits for them, and re-layouts  1.22 us (2%)
    pallas_call x1, Pallas kernels, on_device(): pl.pallas_call(functools.partial(exchange_kernel, devices, narrow_count,...  65.1 us
    pallas_call x1, Pallas kernels, scatter_rows(): pl.pallas_call(functools.partial(scatter_kernel, 16, parts), out_shape=(j...  6.51 us
    sort x1, other arithmetic, on_device(): lax.sort((packed, jnp.where(live > 0, first_key, -1), second_key), num_ke...  4.98 us

profile of v4, /device:TPU:0, one launch (start us, length us, event | category | flops | bytes accessed | tf_op | source)
XLA Modules:
  0.0 79.3 jit_solution(7371762352921870959)
XLA Ops:
  0.6 0.0 copy-start.1
  0.6 0.8 iota_add_fusion
  1.4 0.0 copy-done.1
  1.4 5.0 %sort.21 = (s32[4096]{0:T(1024)S(1)}, s32[4096]{0:T(1024)S(1)}, s32[4096]{0:T(1024)S(1)}) sort(s32[4096]{0:T(1024)S(1)} %get-tuple-element.16, s32[4096]{0:T(1024)S(1)} %get-tuple-element.17, s32[4096]{0:T(1024)S(1)} %copy-done.1), dimensions={0}, to_apply=%region_0.1 | sort | flops 49152 | bytes 98304 | tf_op jit(solution)/shard_map/sort | solution.py:313
  6.4 0.0 copy-start
  6.4 1.2 %copy-done = bf16[4096,128]{1,0:T(8,128)(2,1)S(1)} copy-done((bf16[4096,128]{1,0:T(8,128)(2,1)S(1)}, bf16[4096,128]{1,0:T(8,128)(2,1)}, u32[]{:S(2)}) %copy-start) | copy-done | bytes 1048600
  7.7 65.1 %shard_map.77 = (bf16[32,128,128]{2,1,0:T(8,128)(2,1)S(1)}, s32[8,128]{1,0:T(8,128)S(1)}) custom-call(s32[4096]{0:T(1024)S(1)} %add_select_fusion.order_ref, bf16[4096,128]{1,0:T(8,128)(2,1)S(1)} %copy-done, s32[32,1,128]{2,1,0:T(1,128)S(1)} %bitcast.5, s32[32,1,128]{2,1,0:T(1,128)S(1)} %bitcast.6), custom_call_target="tpu_custom_call" | custom-call | tf_op jit(solution)/shard_map/pallas_call | solution.py:325
  72.8 6.5 %shard_map.78 = (bf16[4096,128]{1,0:T(8,128)(2,1)}, s32[1]{0:T(128)}) custom-call(s32[4096]{0:T(1024)S(1)} %add_select_fusion.order_ref, s32[8,128]{1,0:T(8,128)S(1)} %get-tuple-element.12.dups_ref, bf16[4096,128]{1,0:T(8,128)(2,1)S(1)} %bitcast.4), custom_call_target="tpu_custom_call" | custom-call | tf_op jit(solution)/shard_map/pallas_call | solution.py:84
  (1 shorter events, 0.0 us)
Async XLA Ops:
  0.6 0.8 %copy-start.1 = (s32[4096]{0:T(1024)S(1)}, s32[4096]{0:T(1024)}, u32[]{:S(2)}) copy-start(s32[4096]{0:T(1024)} %param.8) | copy-start | bytes 49156
  6.4 1.2 %copy-start = (bf16[4096,128]{1,0:T(8,128)(2,1)S(1)}, bf16[4096,128]{1,0:T(8,128)(2,1)}, u32[]{:S(2)}) copy-start(bf16[4096,128]{1,0:T(8,128)(2,1)} %payload_any.1) | copy-start | bytes 3145732
